TPU v7x, 32 devices: a whole 2x2x4 slice. The times are simulated.
32 devices in a mesh: band: 4 (over z), sector: 8 (over y, x, core).
Axes of the slice: x: 2, y: 2, z: 4, core: 2. Of those that a mesh axis runs over, the one named last changes fastest.
Arguments:
- field: float32 [2, 640, 2, 2560], P(None, 'band', None, 'sector'), may hold values from -6 to 6
- depart: int32 [2, 640, 80], P(None, 'band', 'sector'), may hold values from -2 to 2
- interp_weight: bfloat16 [2, 640, 80, 64, 32], P(None, 'band', 'sector'), may hold values from -0.75 to 0.75
- legendre: float32 [640, 640, 1281], P('sector', 'band'), may hold values from -0.25 to 0.25
- damping: float32 [2], replicated, may hold values from 0.3 to 30
Outputs:
- new_field: float32 [2, 640, 2, 2560], P(None, 'band', None, 'sector')
All inputs are finite; a program needn't handle non-finite values.
Results may differ from a plain program's by a relative error of at most 0.0003.
Values sent between devices are 32-bit elements; how exact they have to be, the bound alone decides.
No kernel may reach another device: no remote copies, remote signals or barrier semaphores. Data moves between devices by JAX's collectives and lax.ppermute only.
A program may use at most 192 MiB of HBM per device.

v0:
```python
import math
import jax
import jax.numpy as jnp
from jax import lax
from jax.sharding import PartitionSpec as P

HIGHEST = lax.Precision.HIGHEST


def padded(x, sides, width):
    for axis, dim in sides:
        peers, length = (lax.axis_size(axis), x.shape[dim])
        up = [(i, (i + 1) % peers) for i in range(peers)]
        down = [(j, i) for i, j in up]
        last = lax.slice_in_dim(x, length - width, length, axis=dim)
        leading = lax.slice_in_dim(x, 0, width, axis=dim)
        before = lax.ppermute(last, axis, up)
        after = lax.ppermute(leading, axis, down)
        x = jnp.concatenate([before, x, after], axis=dim)
    return x


def phase(product, lon_count):
    return 2.0 * math.pi / lon_count * (product % lon_count).astype(jnp.float32)


def forward_table(lon_count, m_count, pair_total):
    longitude = jnp.arange(lon_count, dtype=jnp.int32)[:, None]
    pair_range = jnp.arange(pair_total, dtype=jnp.int32)[None, :]
    lower_angle = phase(longitude * pair_range, lon_count)
    upper_angle = phase(longitude * (m_count - 1 - pair_range), lon_count)
    table = jnp.stack(
        [jnp.cos(lower_angle), -jnp.sin(lower_angle), jnp.cos(upper_angle), -jnp.sin(upper_angle)],
        axis=1,
    )
    return table / lon_count


def inverse_table(lon_count, m_count, pair_total):
    pair_range = jnp.arange(pair_total, dtype=jnp.int32)[:, None]
    longitude = jnp.arange(lon_count, dtype=jnp.int32)[None, :]
    lower_angle = phase(pair_range * longitude, lon_count)
    upper_angle = phase((m_count - 1 - pair_range) * longitude, lon_count)
    lower_scale = jnp.where(pair_range == 0, 1.0, 2.0)
    return jnp.stack(
        [
            lower_scale * jnp.cos(lower_angle),
            -lower_scale * jnp.sin(lower_angle),
            2.0 * jnp.cos(upper_angle),
            -2.0 * jnp.sin(upper_angle),
        ],
        axis=0,
    )


def pair_masks(pair_index, m_count, row_count):
    column = jnp.arange(row_count, dtype=jnp.int32)[None, :]
    limit = (m_count - pair_index)[:, None]
    leading = column < limit
    lag_value = jnp.where(leading, column, column - limit)
    odd_rows = lag_value % 2 == 1
    degree = jnp.where(leading, pair_index[:, None] + column, column - 1)
    return (leading, odd_rows, degree)


def analyse(wave, legendre, leading, odd_rows):
    stacked = jnp.stack([wave[0] + wave[1], wave[0] - wave[1]])
    product = jnp.einsum("svcpl,plk->svcpk", stacked, legendre, precision=HIGHEST)
    chosen = jnp.where(odd_rows, product[1], product[0])
    return jnp.where(leading, chosen[:, 0:2], chosen[:, 2:4])


def solve_modes(spectrum, damping_levels, degree, m_count):
    ratio = (degree * (degree + 1)).astype(jnp.float32) / float(m_count * m_count)
    return spectrum / (1.0 + damping_levels[:, None, None, None] * ratio[None, None])


def synthesise(spectrum, legendre, leading, odd_rows):
    lower = jnp.where(leading, spectrum, 0.0)
    upper = jnp.where(leading, 0.0, spectrum)
    northern = jnp.concatenate([lower, upper], axis=1)
    southern = jnp.where(odd_rows, -northern, northern)
    stacked = jnp.stack([northern, southern])
    return jnp.einsum("hvcpk,plk->hvcpl", stacked, legendre, precision=HIGHEST)


def advect(field, depart, interp_weight):
    tile_width = interp_weight.shape[-1]
    tile_count = depart.shape[2]
    extended = padded(field, (("sector", 3),), 3 * tile_width)
    pieces = extended.reshape(
        field.shape[0], field.shape[1], field.shape[2], tile_count + 6, tile_width
    )
    window = jnp.zeros(field.shape[:3] + (tile_count, 2 * tile_width), jnp.float32)
    for offset in range(-2, 3):
        lead_part = pieces[:, :, :, 3 + offset : 3 + offset + tile_count]
        next_part = pieces[:, :, :, 4 + offset : 4 + offset + tile_count]
        candidate = jnp.concatenate([lead_part, next_part], axis=4)
        window = jnp.where((depart == offset)[:, :, None, :, None], candidate, window)
    result = jnp.einsum(
        "hlvtj,hltji->hlvti", window, interp_weight.astype(jnp.float32), precision=HIGHEST
    )
    return result.reshape(field.shape)


def local(field, depart, interp_weight, legendre, damping):
    advected = advect(field, depart, interp_weight)
    columns = lax.all_to_all(advected, "sector", split_axis=1, concat_axis=3, tiled=True)
    lon_count = columns.shape[3]
    row_count = legendre.shape[2]
    m_count = row_count - 1
    pair_total = m_count // 2
    fourier = jnp.einsum(
        "hlvn,ncp->hvcpl", columns, forward_table(lon_count, m_count, pair_total), precision=HIGHEST
    )
    wave = lax.all_to_all(fourier, "sector", split_axis=3, concat_axis=4, tiled=True)
    pair_local = legendre.shape[0]
    pair_index = lax.axis_index("sector") * pair_local + jnp.arange(pair_local, dtype=jnp.int32)
    leading, odd_rows, degree = pair_masks(pair_index, m_count, row_count)
    partial_value = analyse(wave, legendre, leading, odd_rows)
    summed = lax.psum(partial_value, "band")
    spectrum = solve_modes(summed, damping, degree, m_count)
    synthesis = synthesise(spectrum, legendre, leading, odd_rows)
    returned = lax.all_to_all(synthesis, "sector", split_axis=4, concat_axis=3, tiled=True)
    gridded = jnp.einsum(
        "hvcpl,cpn->hlvn",
        returned,
        inverse_table(lon_count, m_count, pair_total),
        precision=HIGHEST,
    )
    return lax.all_to_all(gridded, "sector", split_axis=3, concat_axis=1, tiled=True)


def solution(mesh):
    return jax.shard_map(
        local,
        mesh=mesh,
        in_specs=(
            P(None, "band", None, "sector"),
            P(None, "band", "sector"),
            P(None, "band", "sector", None, None),
            P("sector", "band", None),
            P(),
        ),
        out_specs=P(None, "band", None, "sector"),
        check_vma=False,
    )
```

profile of v0, /device:TPU:0, one launch (start us, length us, event | category | flops | bytes accessed | tf_op | source)
XLA Modules:
  0.0 574.6 jit_solution(14221418994076441532)
XLA Ops:
  6.5 1.6 copy.106
  8.2 0.5 collective-permute-start
  8.7 2.9 collective-permute-start.1
  11.6 28.4 %fusion.32 = (f32[2560,1,640]{2,0,1:T(8,128)}, f32[2560,1,640]{2,0,1:T(8,128)}) fusion(s32[640]{0:T(1024)S(1)} %iota_subtract_fusion), kind=kLoop, calls=%fused_computation.40 | loop fusion | flops 16384000 | bytes 13109760 | tf_op jit(solution)/shard_map/cos | solution.py:33
  40.2 47.9 %copy.114 = bf16[2,160,10,64,32]{3,4,2,1,0:T(8,128)(2,1)} copy(bf16[2,160,10,64,32]{1,4,3,2,0:T(8,128)(2,1)} %param.7) | data formatting | bytes 26214400 | tf_op args[2]
  88.2 1.0 fusion.70
  89.3 1.8 maximum_select_fusion
  91.1 3.6 copy.113
  94.7 43.8 %convolution_bitcast_fusion = f32[2,160,2,10,32]{4,2,3,1,0:T(2,128)S(1)} fusion(f32[2,160,2,10,64]{4,2,3,1,0:T(2,128)} %copy.113, bf16[2,160,10,64,32]{3,4,2,1,0:T(8,128)(2,1)} %copy.114), kind=kOutput, calls=%fused_computation.67 | convolution fusion | flops 157286400 | bytes 15564800 | tf_op jit(solution)/shard_map/hlvtj,hltji->hlvti/dot_general | solution.py:100
  138.4 3.4 copy.115
  141.8 2.4 copy.116
  144.2 4.0 all-to-all-start
  148.2 27.9 %sine_negate_fusion.1 = (f32[2560,1,640]{2,0,1:T(8,128)}, f32[2560,1,640]{2,0,1:T(8,128)}) fusion(), kind=kLoop, calls=%fused_computation.41 | loop fusion | flops 16384000 | bytes 13107200 | tf_op jit(solution)/shard_map/neg | solution.py:33
  176.7 19.3 %fusion.54 = f32[2,2,4,640,20]{3,4,1,0,2:T(8,128)S(1)} fusion(f32[2,20,2,2560,1]{3,1,2,0,4:T(8,128)S(1)} %reshape.528, f32[2560,1,640]{2,0,1:T(8,128)} %get-tuple-element.25, f32[2560,1,640]{2,0,1:T(8,128)} %get-tuple-element.24, f32[2560,1,640]{2,0,1:T(8,128)} %get-tuple-element.30, f32[2560,1,640]{2,0,1:T(8,128)} %get-tuple-element.31), kind=kOutput, calls=%fused_computation.78 | convolution fusion | flops 6317670400 | bytes 27852800 | tf_op jit(solution)/shard_map/hlvn,ncp->hvcpl/dot_general | solution.py:113
  196.0 5.0 copy.120
  201.0 10.6 %reshape.535 = f32[8,1,25600]{2,1,0:T(1,128)} reshape(f32[640,4,2,2,20]{4,3,2,1,0:T(2,128)} %bitcast.90) | data formatting | bytes 1638400
  211.6 4.2 all-to-all-start.1
  215.8 1.0 fusion.61
  217.1 11.6 %all-to-all-done.1 = f32[8,1,25600]{2,1,0:T(1,128)S(1)} async-done(((f32[8,1,25600]{2,1,0:T(1,128)}), f32[8,1,25600]{2,1,0:T(1,128)S(1)}, u32[]{:S(2)}, u32[]{:S(2)}) %all-to-all-start.1) | async-done | bytes 819232 | tf_op jit(solution)/shard_map/all_to_all | solution.py:116
  228.7 0.5 broadcast.505
  229.2 2.6 reduce
  231.8 10.9 %reshape.536 = f32[640,4,2,2,20]{4,3,2,1,0:T(2,128)} reshape(f32[8,25600]{1,0:T(8,128)S(1)} %reduce) | data formatting | bytes 1638400
  242.7 6.0 %copy.141 = f32[2,2,4,8,80,20]{4,3,2,5,1,0:T(8,128)S(1)} copy(f32[2,2,4,8,80,20]{5,1,0,2,4,3:T(2,128)} %bitcast.91) | data formatting | bytes 1638400 | tf_op jit(solution)/shard_map/all_to_all | solution.py:116
  250.4 42.7 %fusion.44 = f32[2,2,4,80,1281]{4,2,1,0,3:T(4,128)} fusion(f32[80,160,1281]{2,1,0:T(8,128)} %param.8, f32[2,2,4,80,160]{4,2,1,0,3:T(4,128)S(1)} %fusion.83), kind=kOutput, calls=%fused_computation.61 | convolution fusion | flops 3148185600 | bytes 72965120 | tf_op jit(solution)/shard_map/svcpl,plk->svcpk/dot_general | solution.py:68
  293.2 4.5 fusion.48
  297.6 2.6 slice_select_fusion
  300.3 0.5 multiply_add_fusion
  300.8 28.3 %sine_multiply_fusion.1 = (f32[1,640,2560]{2,1,0:T(8,128)}, f32[1,640,2560]{2,1,0:T(8,128)}) fusion(f32[640]{0:T(1024)S(1)} %fusion.65, f32[640]{0:T(1024)S(1)} %fusion.64), kind=kLoop, calls=%fused_computation.51 | loop fusion | flops 18022400 | bytes 13112320 | tf_op jit(solution)/shard_map/mul | solution.py:48
  329.0 48.0 %all-reduce.2.cloned.1.call-done = f32[2,2,80,1281]{3,1,0,2:T(2,128)} async-done(((f32[2,2,80,1281]{3,1,0,2:T(2,128)}), f32[2,2,80,1281]{3,1,0,2:T(2,128)}) %all-reduce.2.cloned.1.call-update) | async-done | bytes 1639696 | tf_op jit(solution)/shard_map/psum | solution.py:121
  377.0 3.1 broadcast_select_fusion.1
  380.1 1.1 broadcast_select_fusion
  381.3 1.1 fusion.76
  382.4 1.7 maximum_bitcast_fusion.4
  384.1 2.4 negate_select_fusion
  386.5 73.3 %fusion.49 = f32[2,2,4,80,160]{4,2,1,0,3:T(4,128)S(1)} fusion(f32[80,160,1281]{2,1,0:T(8,128)} %param.8, f32[1,2,4,80,1281]{4,2,1,3,0:T(4,128)S(1)} %negate_select_fusion, f32[1,2,4,80,1281]{4,2,1,3,0:T(4,128)S(1)} %maximum_bitcast_fusion.4), kind=kOutput, calls=%fused_computation.77 | convolution fusion | flops 3149825280 | bytes 72965120 | tf_op jit(solution)/shard_map/hvcpk,plk->hvcpl/dot_general | solution.py:84
  459.8 1.7 copy.128
  461.4 4.1 all-to-all-start.2
  465.6 29.7 %cosine_multiply_fusion = (f32[1,640,2560]{2,1,0:T(8,128)}, f32[1,640,2560]{2,1,0:T(8,128)}) fusion(s32[640]{0:T(1024)S(1)} %iota_subtract_fusion), kind=kLoop, calls=%fused_computation.47 | loop fusion | flops 18022400 | bytes 13109760 | tf_op jit(solution)/shard_map/mul | solution.py:49
  495.2 0.8 copy.143
  496.0 0.5 reshape.534
  496.5 19.2 %fusion.47 = f32[2,20,2,2560]{3,1,2,0:T(8,128)S(1)} fusion(f32[2,2,4,640,20]{3,4,2,1,0:T(8,128)S(1)} %reshape.534, f32[1,640,2560]{2,1,0:T(8,128)} %get-tuple-element.23, f32[1,640,2560]{2,1,0:T(8,128)} %get-tuple-element.22, f32[1,640,2560]{2,1,0:T(8,128)} %get-tuple-element.32, f32[1,640,2560]{2,1,0:T(8,128)} %get-tuple-element.33), kind=kOutput, calls=%fused_computation.62 | convolution fusion | flops 6311116800 | bytes 27852800 | tf_op jit(solution)/shard_map/hvcpl,cpn->hlvn/dot_general | solution.py:125
  515.7 5.0 copy.132
  520.7 9.9 %reshape.537 = f32[8,1,25600]{2,1,0:T(1,128)S(1)} reshape(f32[2560,2,2,20]{3,2,1,0:T(2,128)} %bitcast.92) | data formatting | bytes 1638400
  530.6 17.1 %all_to_all.69 = f32[8,1,25600]{2,1,0:T(1,128)S(1)} all-to-all(f32[8,1,25600]{2,1,0:T(1,128)S(1)} %reshape.537), channel_id=1, replica_groups=mesh['band'=4,'sector'=8] {'sector'}, dimensions={0} | all-to-all | bytes 1638400 | tf_op jit(solution)/shard_map/all_to_all | solution.py:131
  547.7 2.6 reduce.1
  550.3 10.9 %reshape.538 = f32[2560,2,2,20]{3,2,1,0:T(2,128)} reshape(f32[8,25600]{1,0:T(8,128)S(1)} %reduce.1) | data formatting | bytes 1638400
  561.1 5.0 copy.144
  566.2 1.5 copy.134
  (34 shorter events, 2.9 us)
Async XLA Ops:
  8.2 79.9 %collective-permute-start = (f32[2,160,2,96]{1,3,2,0:T(8,128)S(1)}, f32[2,160,2,96]{1,3,2,0:T(8,128)S(1)}, u32[]{:S(2)}, u32[]{:S(2)}) collective-permute-start(f32[2,160,2,96]{1,3,2,0:T(8,128)S(1)} %get-tuple-element.15), channel_id=1, source_target_pairs={{0,1},{1,2},{2,3},{3,4},{4,5},{5,6},{6,7},{7,0},{8,9},{9,10},{10,1... | collective-permute-start | bytes 737288 | tf_op jit(solution)/shard_map/ppermute | solution.py:17
  8.7 79.4 %collective-permute-start.1 = (f32[2,160,2,96]{1,3,2,0:T(8,128)S(1)}, f32[2,160,2,96]{1,3,2,0:T(8,128)S(1)}, u32[]{:S(2)}, u32[]{:S(2)}) collective-permute-start(f32[2,160,2,96]{1,3,2,0:T(8,128)S(1)} %get-tuple-element.16), channel_id=1, source_target_pairs={{1,0},{2,1},{3,2},{4,3},{5,4},{6,5},{7,6},{0,7},{9,8},{10,9},{11,1... | collective-permute-start | bytes 737288 | tf_op jit(solution)/shard_map/ppermute | solution.py:18
  11.6 28.4 %copy-start.1 = (s32[2,160,10]{1,0,2:T(2,128)S(1)}, s32[2,160,10]{1,0,2:T(2,128)}, u32[]{:S(2)}) copy-start(s32[2,160,10]{1,0,2:T(2,128)} %param.6) | copy-start | bytes 38404
  144.2 31.9 %all-to-all-start = ((f32[2,160,2,320]{3,2,0,1:T(2,128)}), f32[2,160,2,320]{3,2,0,1:T(2,128)S(1)}, u32[]{:S(2)}, u32[]{:S(2)}) async-start(f32[2,160,2,320]{3,2,0,1:T(2,128)} %copy.116), calls=%async_computation | async-start | bytes 1966080 | tf_op jit(solution)/shard_map/all_to_all | solution.py:108
  211.6 17.1 %all-to-all-start.1 = ((f32[8,1,25600]{2,1,0:T(1,128)}), f32[8,1,25600]{2,1,0:T(1,128)S(1)}, u32[]{:S(2)}, u32[]{:S(2)}) async-start(f32[8,1,25600]{2,1,0:T(1,128)} %reshape.535), calls=%async_computation.1 | async-start | bytes 1638400 | tf_op jit(solution)/shard_map/all_to_all | solution.py:116
  215.8 161.2 %all-reduce.2.cloned.1.call-start = ((), (), s32[]{:S(2)}) async-start(), calls=%async_computation.4 | async-start | bytes 3604480 | tf_op jit(solution)/shard_map/psum | solution.py:121
  250.4 42.8 %copy-start = (pred[80,1281]{1,0:T(8,128)(4,1)S(1)}, pred[80,1281]{1,0:T(8,128)(4,1)}, u32[]{:S(2)}) copy-start(pred[80,1281]{1,0:T(8,128)(4,1)} %get-tuple-element.26) | copy-start | bytes 307444
  297.6 2.7 copy-start.2
  461.4 33.8 %all-to-all-start.2 = ((f32[2,2,4,80,160]{3,2,1,0,4:T(4,128)}), f32[2,2,4,80,160]{3,2,1,0,4:T(4,128)S(1)}, u32[]{:S(2)}, u32[]{:S(2)}) async-start(f32[2,2,4,80,160]{3,2,1,0,4:T(4,128)} %copy.128), calls=%async_computation.2 | async-start | bytes 2621440 | tf_op jit(solution)/shard_map/all_to_all | solution.py:124
Sparse Core Ops, SparseCore 0:
  300.4 76.5 all-reduce.1
where the time goes:
time: 584 us; the launch traced here: 575 us
  matrix products  198 us (34%)
  other arithmetic  140 us (24%)
  local copies, waits for them, and re-layouts  130 us (22%)
  waiting for transfers between devices  59.6 us (10%)
  blocking collectives  17.1 us (3%)
  starting transfers between devices  15.9 us (3%)
  between operations  13.9 us (2%)
    unnamed x12, local copies, waits for them, and re-layouts  91.7 us
    dot_general x1, matrix products, synthesise(): return jnp.einsum('hvcpk,plk->hvcpl', stacked, legendre, precision=HIGHEST)  73.3 us
    psum x1, waiting for transfers between devices, local(): summed = lax.psum(partial_value, 'band')  48 us
    dot_general x1, matrix products, advect(): jnp.einsum('hlvtj,hltji->hlvti', window, interp_weight.astype(jnp.float32...  43.8 us
    dot_general x1, matrix products, analyse(): jnp.einsum('svcpl,plk->svcpk', stacked, legendre, precision=HIGHEST)  42.7 us
    mul x1, other arithmetic, inverse_table(): 2.0 * jnp.cos(upper_angle)  29.7 us
    cos x1, other arithmetic, forward_table(): jnp.cos(upper_angle)  28.4 us
    mul x1, other arithmetic, inverse_table(): -lower_scale * jnp.sin(lower_angle)  28.3 us
  transfers between devices with their start and end apart: 6, of which 2 were waited for; matrix products, arithmetic and copies ran while one was open for 29% of the time, Pallas kernels for 0%

commit v1 on v0

--- a/solution.py
+++ b/solution.py
@@ -3,6 +3,7 @@
 import jax.numpy as jnp
 from jax import lax
 from jax.sharding import PartitionSpec as P
+from jax.lax import all_gather
 
 HIGHEST = lax.Precision.HIGHEST
 
@@ -118,7 +119,7 @@
     pair_index = lax.axis_index("sector") * pair_local + jnp.arange(pair_local, dtype=jnp.int32)
     leading, odd_rows, degree = pair_masks(pair_index, m_count, row_count)
     partial_value = analyse(wave, legendre, leading, odd_rows)
-    summed = lax.psum(partial_value, "band")
+    summed = all_gather(partial_value, "band").sum(axis=0)
     spectrum = solve_modes(summed, damping, degree, m_count)
     synthesis = synthesise(spectrum, legendre, leading, odd_rows)
     returned = lax.all_to_all(synthesis, "sector", split_axis=4, concat_axis=3, tiled=True)

time: 584 us -> 644 us (1.10)
  waiting for transfers between devices: 59.6 us -> 114 us
    all_gather x0 -> x1, waiting for transfers between devices: none -> 101 us  [local(): summed = all_gather(partial_value, 'band').sum(axis=0)]
    psum x1 -> x0, waiting for transfers between devices: 48 us -> none  [local(): summed = lax.psum(partial_value, 'band')]
    reduce_sum x0 -> x1, other arithmetic: none -> 7.08 us  [local(): summed = all_gather(partial_value, 'band').sum(axis=0)]
    unnamed x12 -> x10, local copies, waits for them, and re-layouts: 91.7 us -> 91.8 us
  transfers between devices with their start and end apart: 6 -> 6, of which waited for: 2 -> 2; matrix products, arithmetic and copies ran while one was open for 29% -> 26% of each run, Pallas kernels for 0% -> 0%
where the time goes in v1:
time: 644 us; the launch traced here: 634 us
  matrix products  198 us (31%)
  other arithmetic  145 us (23%)
  local copies, waits for them, and re-layouts  130 us (20%)
  waiting for transfers between devices  114 us (18%)
  blocking collectives  17.2 us (3%)
  starting transfers between devices  15.4 us (2%)
  between operations  14.3 us (2%)
    all_gather x1, waiting for transfers between devices, local(): summed = all_gather(partial_value, 'band').sum(axis=0)  101 us
    unnamed x10, local copies, waits for them, and re-layouts  91.8 us
    dot_general x1, matrix products, synthesise(): return jnp.einsum('hvcpk,plk->hvcpl', stacked, legendre, precision=HIGHEST)  73.2 us
    dot_general x1, matrix products, advect(): jnp.einsum('hlvtj,hltji->hlvti', window, interp_weight.astype(jnp.float32...  43.8 us
    dot_general x1, matrix products, analyse(): jnp.einsum('svcpl,plk->svcpk', stacked, legendre, precision=HIGHEST)  42.7 us
    mul x1, other arithmetic, inverse_table(): 2.0 * jnp.cos(upper_angle)  29.7 us
    cos x1, other arithmetic, forward_table(): jnp.cos(upper_angle)  28.4 us
    mul x1, other arithmetic, inverse_table(): -lower_scale * jnp.sin(lower_angle)  28.4 us
  transfers between devices with their start and end apart: 6, of which 2 were waited for; matrix products, arithmetic and copies ran while one was open for 26% of the time, Pallas kernels for 0%

profile of v1, /device:TPU:0, one launch (start us, length us, event | category | flops | bytes accessed | tf_op | source)
XLA Modules:
  0.0 634.3 jit_solution(6311171368703555158)
XLA Ops:
  6.5 1.6 copy.106
  8.2 0.5 collective-permute-start
  8.7 2.9 collective-permute-start.1
  11.6 28.4 %fusion.32 = (f32[2560,1,640]{2,0,1:T(8,128)}, f32[2560,1,640]{2,0,1:T(8,128)}) fusion(s32[640]{0:T(1024)S(1)} %iota_subtract_fusion), kind=kLoop, calls=%fused_computation.40 | loop fusion | flops 16384000 | bytes 13109760 | tf_op jit(solution)/shard_map/cos | solution.py:34
  40.2 47.9 %copy.114 = bf16[2,160,10,64,32]{3,4,2,1,0:T(8,128)(2,1)} copy(bf16[2,160,10,64,32]{1,4,3,2,0:T(8,128)(2,1)} %param.7) | data formatting | bytes 26214400 | tf_op args[2]
  88.3 1.0 fusion.70
  89.3 1.8 maximum_select_fusion
  91.1 3.6 copy.113
  94.7 43.8 %convolution_bitcast_fusion = f32[2,160,2,10,32]{4,2,3,1,0:T(2,128)S(1)} fusion(f32[2,160,2,10,64]{4,2,3,1,0:T(2,128)} %copy.113, bf16[2,160,10,64,32]{3,4,2,1,0:T(8,128)(2,1)} %copy.114), kind=kOutput, calls=%fused_computation.67 | convolution fusion | flops 157286400 | bytes 15564800 | tf_op jit(solution)/shard_map/hlvtj,hltji->hlvti/dot_general | solution.py:101
  138.5 3.4 copy.115
  141.9 2.4 copy.116
  144.2 3.7 all-to-all-start
  148.0 27.9 %sine_negate_fusion.1 = (f32[2560,1,640]{2,0,1:T(8,128)}, f32[2560,1,640]{2,0,1:T(8,128)}) fusion(), kind=kLoop, calls=%fused_computation.41 | loop fusion | flops 16384000 | bytes 13107200 | tf_op jit(solution)/shard_map/neg | solution.py:34
  176.5 19.3 %fusion.54 = f32[2,2,4,640,20]{3,4,1,0,2:T(8,128)S(1)} fusion(f32[2,20,2,2560,1]{3,1,2,0,4:T(8,128)S(1)} %reshape.511, f32[2560,1,640]{2,0,1:T(8,128)} %get-tuple-element.25, f32[2560,1,640]{2,0,1:T(8,128)} %get-tuple-element.24, f32[2560,1,640]{2,0,1:T(8,128)} %get-tuple-element.30, f32[2560,1,640]{2,0,1:T(8,128)} %get-tuple-element.31), kind=kOutput, calls=%fused_computation.78 | convolution fusion | flops 6317670400 | bytes 27852800 | tf_op jit(solution)/shard_map/hlvn,ncp->hvcpl/dot_general | solution.py:114
  195.8 5.0 copy.120
  200.8 10.6 %reshape.518 = f32[8,1,25600]{2,1,0:T(1,128)} reshape(f32[640,4,2,2,20]{4,3,2,1,0:T(2,128)} %bitcast.91) | data formatting | bytes 1638400
  211.4 4.2 all-to-all-start.1
  216.0 12.5 %all-to-all-done.1 = f32[8,1,25600]{2,1,0:T(1,128)S(1)} async-done(((f32[8,1,25600]{2,1,0:T(1,128)}), f32[8,1,25600]{2,1,0:T(1,128)S(1)}, u32[]{:S(2)}, u32[]{:S(2)}) %all-to-all-start.1) | async-done | bytes 819232 | tf_op jit(solution)/shard_map/all_to_all | solution.py:117
  228.5 0.5 broadcast.559
  229.0 2.6 reduce
  231.6 10.9 %reshape.519 = f32[640,4,2,2,20]{4,3,2,1,0:T(2,128)} reshape(f32[8,25600]{1,0:T(8,128)S(1)} %reduce) | data formatting | bytes 1638400
  242.5 6.2 copy.141
  250.4 42.7 %fusion.44 = f32[2,2,4,80,1281]{4,2,1,0,3:T(4,128)} fusion(f32[80,160,1281]{2,1,0:T(8,128)} %param.8, f32[2,2,4,80,160]{4,2,1,0,3:T(4,128)S(1)} %fusion.83), kind=kOutput, calls=%fused_computation.61 | convolution fusion | flops 3148185600 | bytes 72965120 | tf_op jit(solution)/shard_map/svcpl,plk->svcpk/dot_general | solution.py:69
  293.1 4.5 fusion.48
  297.6 2.7 slice_select_fusion
  300.5 0.5 multiply_add_fusion
  301.0 28.4 %sine_multiply_fusion.1 = (f32[1,640,2560]{2,1,0:T(8,128)}, f32[1,640,2560]{2,1,0:T(8,128)}) fusion(f32[640]{0:T(1024)S(1)} %fusion.65, f32[640]{0:T(1024)S(1)} %fusion.64), kind=kLoop, calls=%fused_computation.51 | loop fusion | flops 18022400 | bytes 13112320 | tf_op jit(solution)/shard_map/mul | solution.py:49
  329.4 101.4 %all-gather.3.cloned.1.call-done = f32[8,2,80,1281]{3,1,0,2:T(2,128)} async-done(((f32[2,2,80,1281]{3,1,0,2:T(2,128)}), f32[8,2,80,1281]{3,1,0,2:T(2,128)}) %all-gather.3.cloned.1.call-update) | async-done | bytes 6558736 | tf_op jit(solution)/shard_map/all_gather | solution.py:122
  430.8 7.1 %reduce_sum.9 = f32[2,2,80,1281]{3,1,0,2:T(2,128)S(1)} reduce(f32[4,2,2,80,1281]{4,2,1,0,3:T(2,128)} %bitcast.96, f32[]{:T(128)} %constant.78.clone.1), dimensions={0}, to_apply=%region_0.1 | reduce | flops 1229760 | bytes 8198404 | tf_op jit(solution)/shard_map/reduce_sum | solution.py:122
  437.9 1.7 broadcast_select_fusion.1
  439.6 1.1 broadcast_select_fusion
  440.8 1.1 fusion.76
  441.9 1.7 maximum_bitcast_fusion.4
  443.6 2.4 negate_select_fusion
  446.0 73.2 %fusion.49 = f32[2,2,4,80,160]{4,2,1,0,3:T(4,128)S(1)} fusion(f32[80,160,1281]{2,1,0:T(8,128)} %param.8, f32[1,2,4,80,1281]{4,2,1,3,0:T(4,128)S(1)} %negate_select_fusion, f32[1,2,4,80,1281]{4,2,1,3,0:T(4,128)S(1)} %maximum_bitcast_fusion.4), kind=kOutput, calls=%fused_computation.77 | convolution fusion | flops 3149825280 | bytes 72965120 | tf_op jit(solution)/shard_map/hvcpk,plk->hvcpl/dot_general | solution.py:85
  519.2 1.6 copy.128
  520.8 3.9 all-to-all-start.2
  524.8 29.7 %cosine_multiply_fusion = (f32[1,640,2560]{2,1,0:T(8,128)}, f32[1,640,2560]{2,1,0:T(8,128)}) fusion(s32[640]{0:T(1024)S(1)} %iota_subtract_fusion), kind=kLoop, calls=%fused_computation.47 | loop fusion | flops 18022400 | bytes 13109760 | tf_op jit(solution)/shard_map/mul | solution.py:50
  554.5 0.8 copy.143
  555.2 0.5 reshape.517
  555.7 19.2 %fusion.47 = f32[2,20,2,2560]{3,1,2,0:T(8,128)S(1)} fusion(f32[2,2,4,640,20]{3,4,2,1,0:T(8,128)S(1)} %reshape.517, f32[1,640,2560]{2,1,0:T(8,128)} %get-tuple-element.23, f32[1,640,2560]{2,1,0:T(8,128)} %get-tuple-element.22, f32[1,640,2560]{2,1,0:T(8,128)} %get-tuple-element.32, f32[1,640,2560]{2,1,0:T(8,128)} %get-tuple-element.33), kind=kOutput, calls=%fused_computation.62 | convolution fusion | flops 6311116800 | bytes 27852800 | tf_op jit(solution)/shard_map/hvcpl,cpn->hlvn/dot_general | solution.py:126
  574.9 4.9 copy.132
  579.9 9.9 %reshape.520 = f32[8,1,25600]{2,1,0:T(1,128)S(1)} reshape(f32[2560,2,2,20]{3,2,1,0:T(2,128)} %bitcast.93) | data formatting | bytes 1638400
  589.8 17.2 %all_to_all.69 = f32[8,1,25600]{2,1,0:T(1,128)S(1)} all-to-all(f32[8,1,25600]{2,1,0:T(1,128)S(1)} %reshape.520), channel_id=1, replica_groups=mesh['band'=4,'sector'=8] {'sector'}, dimensions={0} | all-to-all | bytes 1638400 | tf_op jit(solution)/shard_map/all_to_all | solution.py:132
  607.0 2.6 reduce.1
  609.5 10.9 %reshape.521 = f32[2560,2,2,20]{3,2,1,0:T(2,128)} reshape(f32[8,25600]{1,0:T(8,128)S(1)} %reduce.1) | data formatting | bytes 1638400
  620.4 5.0 copy.144
  625.5 1.5 copy.134
  (33 shorter events, 3.2 us)
Async XLA Ops:
  8.2 80.0 %collective-permute-start = (f32[2,160,2,96]{1,3,2,0:T(8,128)S(1)}, f32[2,160,2,96]{1,3,2,0:T(8,128)S(1)}, u32[]{:S(2)}, u32[]{:S(2)}) collective-permute-start(f32[2,160,2,96]{1,3,2,0:T(8,128)S(1)} %get-tuple-element.15), channel_id=1, source_target_pairs={{0,1},{1,2},{2,3},{3,4},{4,5},{5,6},{6,7},{7,0},{8,9},{9,10},{10,1... | collective-permute-start | bytes 737288 | tf_op jit(solution)/shard_map/ppermute | solution.py:18
  8.7 79.4 %collective-permute-start.1 = (f32[2,160,2,96]{1,3,2,0:T(8,128)S(1)}, f32[2,160,2,96]{1,3,2,0:T(8,128)S(1)}, u32[]{:S(2)}, u32[]{:S(2)}) collective-permute-start(f32[2,160,2,96]{1,3,2,0:T(8,128)S(1)} %get-tuple-element.16), channel_id=1, source_target_pairs={{1,0},{2,1},{3,2},{4,3},{5,4},{6,5},{7,6},{0,7},{9,8},{10,9},{11,1... | collective-permute-start | bytes 737288 | tf_op jit(solution)/shard_map/ppermute | solution.py:19
  11.6 28.4 %copy-start = (s32[2,160,10]{1,0,2:T(2,128)S(1)}, s32[2,160,10]{1,0,2:T(2,128)}, u32[]{:S(2)}) copy-start(s32[2,160,10]{1,0,2:T(2,128)} %param.6) | copy-start | bytes 38404
  144.2 31.6 %all-to-all-start = ((f32[2,160,2,320]{3,2,0,1:T(2,128)}), f32[2,160,2,320]{3,2,0,1:T(2,128)S(1)}, u32[]{:S(2)}, u32[]{:S(2)}) async-start(f32[2,160,2,320]{3,2,0,1:T(2,128)} %copy.116), calls=%async_computation | async-start | bytes 1966080 | tf_op jit(solution)/shard_map/all_to_all | solution.py:109
  211.4 17.1 %all-to-all-start.1 = ((f32[8,1,25600]{2,1,0:T(1,128)}), f32[8,1,25600]{2,1,0:T(1,128)S(1)}, u32[]{:S(2)}, u32[]{:S(2)}) async-start(f32[8,1,25600]{2,1,0:T(1,128)} %reshape.518), calls=%async_computation.1 | async-start | bytes 1638400 | tf_op jit(solution)/shard_map/all_to_all | solution.py:117
  215.6 215.2 %all-gather.3.cloned.1.call-start = ((), (), s32[]{:S(2)}) async-start(), calls=%async_computation.4 | async-start | bytes 9011200 | tf_op jit(solution)/shard_map/all_gather | solution.py:122
  297.5 3.0 copy-start.1
  520.8 33.6 %all-to-all-start.2 = ((f32[2,2,4,80,160]{3,2,1,0,4:T(4,128)}), f32[2,2,4,80,160]{3,2,1,0,4:T(4,128)S(1)}, u32[]{:S(2)}, u32[]{:S(2)}) async-start(f32[2,2,4,80,160]{3,2,1,0,4:T(4,128)} %copy.128), calls=%async_computation.2 | async-start | bytes 2621440 | tf_op jit(solution)/shard_map/all_to_all | solution.py:125
Sparse Core Ops, SparseCore 0:
  300.4 130.3 all-gather.2
